TPU v7x, 32 devices: a whole 2x2x4 slice. The times are simulated.
32 devices in a mesh: batch: 8 (over z, y), mp: 4 (over x, core).
Axes of the slice: x: 2, y: 2, z: 4, core: 2. Of those that a mesh axis runs over, the one named last changes fastest.
Arguments:
- init_state: float32 [4096, 256], P(('batch', 'mp')), may hold values from -6 to 6
- brownian: bfloat16 [32, 4096, 256], P(None, ('batch', 'mp')), may hold values from -6 to 6
- step_size: float32 [4096], P(('batch', 'mp')), may hold values from 0.02 to 0.1
- lengths: int32 [4096], P(('batch', 'mp')), may hold values from 1 to 32, as said below
- obs_steps: int32 [4096, 8], P(('batch', 'mp')), may hold values from 1 to 32, as said below
- observed: bfloat16 [4096, 8, 128], P(('batch', 'mp')), may hold values from -6 to 6
- w_in: bfloat16 [256, 1024], P(None, 'mp'), may hold values from -0.375 to 0.375
- b_in: bfloat16 [1024], P('mp'), may hold values from -3 to 3
- w_out: bfloat16 [1024, 256], P('mp'), may hold values from -0.1875 to 0.1875
- b_out: float32 [256], replicated, may hold values from -4 to 4
- decoder: bfloat16 [256, 128], replicated, may hold values from -0.375 to 0.375
- prior_rate: float32 [256], replicated, may hold values from 0.1 to 2
- diffusion: float32 [256], replicated, may hold values from 0.7 to 1.4
Outputs:
- elbo_series: float32 [4096], P(('batch', 'mp'))
- scores: float32 [2], replicated
- grad_w_in: float32 [256, 1024], P(None, 'mp')
- grad_b_in: float32 [1024], P('mp')
- grad_w_out: float32 [1024, 256], P('mp')
- grad_b_out: float32 [256], replicated
- grad_decoder: float32 [256, 128], replicated
- grad_init: float32 [4096, 256], P(('batch', 'mp'))
Inputs may be any that keep to these rules, and one draw needn't show every extreme that they name: `lengths`: some series has 32 live steps in every draw. obs_steps[i, j] is at most lengths[i].
All inputs are finite; a program needn't handle non-finite values.
Results may differ from a plain program's by a relative error of at most 0.0019.
Values may be sent and summed in bfloat16 or wider, within the bound.
A program may use at most 64 MiB of HBM per device.

v0:
```python
import jax
import jax.numpy as jnp
from jax import lax
from jax.sharding import PartitionSpec as P


def solve(
    init_state,
    brownian,
    step_size,
    lengths,
    obs_steps,
    observed,
    horizon,
    w_in_all,
    b_in_all,
    w_out_all,
    b_out,
    decoder,
    prior_rate,
    diffusion,
):
    row_count = init_state.shape[0]
    num_steps = brownian.shape[0]
    latent_width = init_state.shape[1]
    hidden_width = w_in_all.shape[1]
    step_col = step_size[:, None]
    root_col = jnp.sqrt(step_size)[:, None]
    bias_in = b_in_all.astype(jnp.float32)

    def forward(step_index, loop_state):
        trajectory, activities, residuals, kl_sum = loop_state
        current = lax.dynamic_index_in_dim(trajectory, step_index, 0, keepdims=False)
        increment = lax.dynamic_index_in_dim(brownian, step_index, 0, keepdims=False)
        live_now = (step_index < lengths).astype(jnp.float32)
        activity = jnp.tanh(
            jnp.dot(current.astype(jnp.bfloat16), w_in_all, preferred_element_type=jnp.float32)
            + bias_in
        ).astype(jnp.bfloat16)
        drift_now = jnp.dot(activity, w_out_all, preferred_element_type=jnp.float32) + b_out
        residual = (drift_now + prior_rate * current) / diffusion
        kl_sum = kl_sum + live_now * 0.5 * step_size * jnp.sum(residual * residual, axis=1)
        following = current + live_now[:, None] * (
            step_col * drift_now + diffusion * root_col * increment.astype(jnp.float32)
        )
        trajectory = lax.dynamic_update_index_in_dim(trajectory, following, step_index + 1, 0)
        activities = lax.dynamic_update_index_in_dim(activities, activity, step_index, 0)
        residuals = lax.dynamic_update_index_in_dim(residuals, residual, step_index, 0)
        return (trajectory, activities, residuals, kl_sum)

    start_path = lax.dynamic_update_index_in_dim(
        jnp.zeros((num_steps + 1, row_count, latent_width), jnp.float32), init_state, 0, 0
    )
    start_forward = (
        start_path,
        jnp.zeros((num_steps, row_count, hidden_width), jnp.bfloat16),
        jnp.zeros((num_steps, row_count, latent_width), jnp.float32),
        jnp.zeros((row_count,), jnp.float32),
    )
    trajectory, activities, residuals, kl_total = lax.fori_loop(0, horizon, forward, start_forward)
    picked = trajectory[obs_steps, jnp.arange(row_count, dtype=jnp.int32)[:, None]]
    picked_round = picked.astype(jnp.bfloat16).reshape(-1, latent_width)
    flat_obs = observed.reshape(-1, observed.shape[2]).astype(jnp.float32)
    misfit = jnp.dot(picked_round, decoder, preferred_element_type=jnp.float32) - flat_obs
    loglik = -0.5 * jnp.sum((misfit * misfit).reshape(row_count, -1), axis=1)
    misfit_round = misfit.astype(jnp.bfloat16)
    decoder_grad = jnp.dot(picked_round.T, misfit_round, preferred_element_type=jnp.float32)
    misfit_back = jnp.dot(misfit_round, decoder.T, preferred_element_type=jnp.float32).reshape(
        row_count, obs_steps.shape[1], latent_width
    )
    onehot = (
        obs_steps[:, :, None] == jnp.arange(num_steps + 1, dtype=jnp.int32)[None, None, :]
    ).astype(jnp.float32)
    obs_back = jnp.einsum("bjs,bjl->sbl", onehot, misfit_back, precision=lax.Precision.HIGHEST)

    def backward(back_index, loop_state):
        cotangent, sum_w_in, sum_b_in, sum_w_out, sum_b_out = loop_state
        step_index = horizon - 1 - back_index
        current = lax.dynamic_index_in_dim(trajectory, step_index, 0, keepdims=False)
        activity = lax.dynamic_index_in_dim(activities, step_index, 0, keepdims=False)
        residual = lax.dynamic_index_in_dim(residuals, step_index, 0, keepdims=False)
        obs_here = lax.dynamic_index_in_dim(obs_back, step_index, 0, keepdims=False)
        live_now = (step_index < lengths).astype(jnp.float32)
        factor = (live_now * step_size)[:, None]
        scaled = residual / diffusion
        update = factor * (cotangent + scaled)
        update_round = update.astype(jnp.bfloat16)
        activity_value = activity.astype(jnp.float32)
        pre_grad = jnp.dot(update_round, w_out_all.T, preferred_element_type=jnp.float32) * (
            1.0 - activity_value * activity_value
        )
        pre_round = pre_grad.astype(jnp.bfloat16)
        cotangent = (
            cotangent
            + factor * prior_rate * scaled
            + jnp.dot(pre_round, w_in_all.T, preferred_element_type=jnp.float32)
            + obs_here
        )
        sum_w_in = sum_w_in + jnp.dot(
            current.astype(jnp.bfloat16).T, pre_round, preferred_element_type=jnp.float32
        )
        sum_b_in = sum_b_in + jnp.sum(pre_grad, axis=0)
        sum_w_out = sum_w_out + jnp.dot(
            activity.T, update_round, preferred_element_type=jnp.float32
        )
        sum_b_out = sum_b_out + jnp.sum(update, axis=0)
        return (cotangent, sum_w_in, sum_b_in, sum_w_out, sum_b_out)

    start_back = (
        lax.dynamic_index_in_dim(obs_back, horizon, 0, keepdims=False),
        jnp.zeros((latent_width, hidden_width), jnp.float32),
        jnp.zeros((hidden_width,), jnp.float32),
        jnp.zeros((hidden_width, latent_width), jnp.float32),
        jnp.zeros((latent_width,), jnp.float32),
    )
    cotangent, sum_w_in, sum_b_in, sum_w_out, sum_b_out = lax.fori_loop(
        0, horizon, backward, start_back
    )
    divisor = (latent_width * lengths + observed.shape[2] * obs_steps.shape[1]).astype(jnp.float32)
    elbo_rows = (loglik - kl_total) / divisor
    return (
        elbo_rows,
        cotangent,
        jnp.sum(loglik),
        jnp.sum(kl_total),
        sum_w_in,
        sum_b_in,
        sum_w_out,
        sum_b_out,
        decoder_grad,
    )


def on_device(
    init_state,
    brownian,
    step_size,
    lengths,
    obs_steps,
    observed,
    w_in,
    b_in,
    w_out,
    b_out,
    decoder,
    prior_rate,
    diffusion,
):
    w_in_all, w_out_all, b_in_all = (
        lax.all_gather(w_in, "mp", axis=1, tiled=True),
        lax.all_gather(w_out, "mp", axis=0, tiled=True),
        lax.all_gather(b_in, "mp", axis=0, tiled=True),
    )
    row_count = init_state.shape[0]
    num_steps = brownian.shape[0]
    hidden_width = w_in_all.shape[1]
    shared = (w_in_all, b_in_all, w_out_all, b_out, decoder, prior_rate, diffusion)
    outcome = solve(
        init_state, brownian, step_size, lengths, obs_steps, observed, num_steps, *shared
    )
    (
        elbo_series,
        cotangent,
        loglik_local,
        kl_local,
        sum_w_in,
        sum_b_in,
        sum_w_out,
        sum_b_out,
        decoder_grad,
    ) = outcome
    loglik_all, kl_all = lax.psum((loglik_local, kl_local), ("batch", "mp"))
    total_series = row_count * lax.axis_size("batch") * lax.axis_size("mp")
    share = hidden_width // lax.axis_size("mp")
    offset = lax.axis_index("mp") * share
    all_w_in, all_b_in, all_w_out, all_b_out, all_decoder = lax.psum(
        (sum_w_in, sum_b_in, sum_w_out, sum_b_out, decoder_grad), ("batch", "mp")
    )
    own_w_in = lax.dynamic_slice_in_dim(all_w_in, offset, share, 1)
    own_b_in = lax.dynamic_slice_in_dim(all_b_in, offset, share, 0)
    own_w_out = lax.dynamic_slice_in_dim(all_w_out, offset, share, 0)
    scores = jnp.stack([loglik_all / total_series, kl_all / total_series])
    return (
        elbo_series,
        scores,
        own_w_in / total_series,
        own_b_in / total_series,
        own_w_out / total_series,
        all_b_out / total_series,
        all_decoder / total_series,
        cotangent,
    )


def solution(mesh):
    placed = (
        P(("batch", "mp"), None),
        P(None, ("batch", "mp"), None),
        P(("batch", "mp")),
        P(("batch", "mp")),
        P(("batch", "mp"), None),
        P(("batch", "mp"), None, None),
        P(None, "mp"),
        P("mp"),
        P("mp", None),
        P(),
        P(),
        P(),
        P(),
    )
    return jax.shard_map(
        on_device,
        mesh=mesh,
        in_specs=placed,
        out_specs=(
            P(("batch", "mp")),
            P(),
            P(None, "mp"),
            P("mp"),
            P("mp", None),
            P(),
            P(),
            P(("batch", "mp"), None),
        ),
        check_vma=False,
    )
```

profile of v0, /device:TPU:25, one launch (start us, length us, event | category | flops | bytes accessed | tf_op | source)
XLA Modules:
  0.0 914.3 jit_solution(16024416329355499509)
XLA Ops:
  8.8 7.9 all_gather.11
  16.7 7.5 all_gather.9
  24.8 5.0 all-gather
  30.6 3.4 dynamic_update_slice.37
  34.0 372.4 %while.46 = (s32[]{:T(128)}, f32[33,128,256]{2,1,0:T(8,128)}, bf16[32,128,1024]{2,1,0:T(8,128)(2,1)}, f32[32,128,256]{2,1,0:T(8,128)}, f32[128]{0:T(128)}, /*ind...) while((s32[]{:T(128)}, f32[33,128,256]{2,1,0:T(8,128)}, ...), condition=%wide.region_2.3_spmd.clone, body=%wide.region_0.2_spmd.clone.sunk | while | flops 135005056 | bytes 20398324 | solution.py:60
  37.4 2.2 copy.43
  42.4 2.0 copy.55
  49.0 2.2 copy.43
  60.6 2.2 copy.43
  65.6 2.0 copy.55
  72.3 2.2 copy.43
  77.3 2.0 copy.55
  83.9 2.2 copy.43
  88.9 2.0 copy.55
  95.6 2.2 copy.43
  100.5 2.0 copy.55
  107.2 2.2 copy.43
  112.2 2.0 copy.55
  118.8 2.2 copy.43
  130.5 2.2 copy.43
  135.5 2.0 copy.55
  142.1 2.2 copy.43
  147.1 2.0 copy.55
  153.7 2.2 copy.43
  158.7 2.0 copy.55
  165.4 2.2 copy.43
  170.4 2.0 copy.55
  177.1 2.2 copy.43
  182.0 2.0 copy.55
  188.7 2.2 copy.43
  193.7 2.0 copy.55
  200.3 2.2 copy.43
  205.3 2.0 copy.55
  211.9 2.2 copy.43
  223.6 2.2 copy.43
  228.5 2.0 copy.55
  235.2 2.2 copy.43
  246.8 2.2 copy.43
  251.8 2.0 copy.55
  258.4 2.2 copy.43
  263.4 2.0 copy.55
  270.1 2.2 copy.43
  275.1 2.0 copy.55
  281.7 2.2 copy.43
  293.4 2.2 copy.43
  298.4 2.0 copy.55
  305.0 2.2 copy.43
  316.7 2.2 copy.43
  328.3 2.2 copy.43
  340.0 2.2 copy.43
  351.6 2.2 copy.43
  363.2 2.2 copy.43
  374.8 2.2 copy.43
  386.5 2.2 copy.43
  398.1 2.2 copy.43
  406.5 3.9 convert.36
  410.5 17.4 %gather_fusion = bf16[1024,256]{1,0:T(8,128)(2,1)} fusion(f32[33,128,256]{2,1,0:T(8,128)} %get-tuple-element.954, s32[1024]{0:T(1024)S(1)} %reshape.63), kind=kCustom, calls=%fused_computation | custom fusion | bytes 1056768 | tf_op jit(solution)/shard_map/gather | solution.py:61
  428.7 2.1 copy.29
  430.9 2.1 multiply_reduce_fusion.1
  433.3 2.0 fusion.25
  435.3 2.9 fusion.23
  440.6 327.9 %while.47 = (s32[]{:T(128)}, f32[128,256]{1,0:T(8,128)}, f32[256,1024]{1,0:T(8,128)S(1)}, f32[1024]{0:T(1024)S(1)}, f32[1024,256]{1,0:T(8,128)S(1)}, /*index=5*/...) while((s32[]{:T(128)}, f32[128,256]{1,0:T(8,128)}, ...), condition=%wide.region_12.13_spmd.clone, body=%wide.region_9.12_spmd.clone.sunk | while | flops 270632448 | bytes 7899009 | solution.py:116
  772.6 38.4 %all-reduce.1 = (f32[]{:T(128)}, f32[]{:T(128)}, f32[1024]{0:T(1024)S(1)}, f32[256]{0:T(256)S(1)}) all-reduce(f32[]{:T(128)} %get-tuple-element.1005, f32[]{:T(128)} %get-tuple-element.1003, f32[1024]{0:T(1024)S(1)} %get-tuple-element.769, f32[256]{0:T(256)} %get-tuple-element.771), channel_id=1, replica_groups=mesh['batch'=8,'mp'=4] {'batch','mp'}, use_global_device_ids=true, to_apply=%region_8.9 | all-reduce | flops 1282 | bytes 10256 | tf_op jit(solution)/shard_map/psum | solution.py:172
  813.5 90.5 %all-reduce.5.cloned.1.call-done = (f32[256,1024]{1,0:T(8,128)}, f32[1024,256]{1,0:T(8,128)}, f32[256,128]{1,0:T(8,128)}) async-done(((f32[256,1024]{1,0:T(8,128)}, f32[1024,256]{1,0:T(8,128)}, f32[256,128]{1,0:T(8,128)}), (f32[256,1024]{1,0:T(8,128)}, f32[1024,256]{1,0:T(8,128)}, f32[256,128]{1,0:T(8,128)})) %all-reduce.5.cloned.1.call-update) | async-done | bytes 2228240 | tf_op jit(solution)/shard_map/psum | solution.py:176
  (729 shorter events, 605.4 us)
Async XLA Ops:
  7.2 423.7 %copy-start = (bf16[256,128]{1,0:T(8,128)(2,1)S(1)}, bf16[256,128]{1,0:T(8,128)(2,1)}, u32[]{:S(2)}) copy-start(bf16[256,128]{1,0:T(8,128)(2,1)} %param.27) | copy-start | bytes 196612
  7.2 26.8 %copy-start.10 = (f32[256]{0:T(256)S(1)}, f32[256]{0:T(256)}, u32[]{:S(2)}) copy-start(f32[256]{0:T(256)} %param.26) | copy-start | bytes 3076
  7.2 26.8 %copy-start.8 = (f32[256]{0:T(256)S(1)}, f32[256]{0:T(256)}, u32[]{:S(2)}) copy-start(f32[256]{0:T(256)} %param.28) | copy-start | bytes 3076
  7.2 26.8 %copy-start.5 = (f32[256]{0:T(256)S(1)}, f32[256]{0:T(256)}, u32[]{:S(2)}) copy-start(f32[256]{0:T(256)} %param.29) | copy-start | bytes 3076
  7.2 896.8 %all-reduce.5.cloned.1.call-start = ((), (), s32[]{:S(2)}) async-start(), calls=%async_computation | async-start | bytes 4456448 | tf_op jit(solution)/shard_map/psum | solution.py:176
  406.5 21.3 %copy-start.4 = (bf16[128,8,128]{2,1,0:T(8,128)(2,1)S(1)}, bf16[128,8,128]{2,1,0:T(8,128)(2,1)}, u32[]{:S(2)}) copy-start(bf16[128,8,128]{2,1,0:T(8,128)(2,1)} %param.22) | copy-start | bytes 786436
  443.7 4.0 copy-start.7
  443.7 4.0 copy-start.9
  453.3 4.0 copy-start.7
  453.3 4.0 copy-start.9
  463.5 4.0 copy-start.7
  463.5 4.0 copy-start.9
  473.8 4.0 copy-start.7
  473.8 4.0 copy-start.9
  484.1 4.0 copy-start.7
  484.1 4.0 copy-start.9
  494.3 4.0 copy-start.7
  494.4 4.0 copy-start.9
  504.6 4.0 copy-start.7
  504.6 4.0 copy-start.9
  514.9 4.0 copy-start.7
  514.9 4.0 copy-start.9
  525.2 4.0 copy-start.7
  525.2 4.0 copy-start.9
  535.4 4.0 copy-start.7
  535.4 4.0 copy-start.9
  545.7 4.0 copy-start.7
  545.7 4.0 copy-start.9
  556.0 4.0 copy-start.7
  556.0 4.0 copy-start.9
  566.2 4.0 copy-start.7
  566.2 4.0 copy-start.9
  576.5 4.0 copy-start.7
  576.5 4.0 copy-start.9
  586.8 4.0 copy-start.7
  586.8 4.0 copy-start.9
  597.0 4.0 copy-start.7
  597.1 4.0 copy-start.9
  607.3 4.0 copy-start.7
  607.3 4.0 copy-start.9
  617.6 4.0 copy-start.7
  617.6 4.0 copy-start.9
  627.8 4.0 copy-start.7
  627.9 4.0 copy-start.9
  638.1 4.0 copy-start.7
  648.4 4.0 copy-start.7
  648.4 4.0 copy-start.9
  658.7 4.0 copy-start.7
  668.9 4.0 copy-start.7
  668.9 4.0 copy-start.9
  679.2 4.0 copy-start.7
  689.5 4.0 copy-start.7
  689.5 4.0 copy-start.9
  699.7 4.0 copy-start.7
  710.0 4.0 copy-start.7
  710.0 4.0 copy-start.9
  720.3 4.0 copy-start.7
  720.3 4.0 copy-start.9
  730.5 4.0 copy-start.7
  730.6 4.0 copy-start.9
  740.8 4.0 copy-start.7
  751.1 4.0 copy-start.7
  751.1 4.0 copy-start.9
  761.4 4.0 copy-start.7
  (41 other events, 63.1 us)
Sparse Core Ops, SparseCore 0:
  770.0 133.9 all-reduce.4
where the time goes:
time: 931 us; the launch traced here: 914 us
  matrix products  310 us (33%)
  local copies, waits for them, and re-layouts  237 us (25%)
  other arithmetic  199 us (21%)
  waiting for transfers between devices  90.5 us (10%)
  blocking collectives  58.8 us (6%)
  between operations  15.5 us (2%)
    while x256, local copies, waits for them, and re-layouts  136 us
    psum x1, waiting for transfers between devices, on_device(): lax.psum((sum_w_in, sum_b_in, sum_w_out, sum_b_out, decoder_grad), ('batc...  90.5 us
    dot_general x32, matrix products, backward(): jnp.dot(pre_round, w_in_all.T, preferred_element_type=jnp.float32)  62.3 us
    dot_general x32, matrix products, forward(): jnp.dot(current.astype(jnp.bfloat16), w_in_all, preferred_element_type=jn...  59.5 us
    dot_general x32, matrix products, forward(): jnp.dot(activity, w_out_all, preferred_element_type=jnp.float32) + b_out  55.7 us
    dot_general x32, matrix products, backward(): jnp.dot(activity.T, update_round, preferred_element_type=jnp.float32)  44.8 us
    dynamic_slice x32, local copies, waits for them, and re-layouts, backward(): obs_here = lax.dynamic_index_in_dim(obs_back, step_index, 0, keepdims=False)  42.4 us
    dot_general x32, matrix products, backward(): jnp.dot(update_round, w_out_all.T, preferred_element_type=jnp.float32)  40.7 us
  transfers between devices with their start and end apart: 1, of which 1 were waited for; matrix products, arithmetic and copies ran while one was open for 0% of the time, Pallas kernels for 0%

commit v1 on v0

v1 whole, which is shorter than its diff:
```python
import jax
import jax.numpy as jnp
from jax import lax
from jax.experimental import pallas as pl
from jax.experimental.pallas import tpu as pltpu
from jax.sharding import PartitionSpec as P

F32 = jnp.float32
BF16 = jnp.bfloat16
NT = (((1,), (1,)), ((), ()))


def dot(a, b):
    return jnp.dot(a, b, preferred_element_type=F32)


def dot_nt(a, b):
    return lax.dot_general(a, b, NT, preferred_element_type=F32)


def fold(value):
    return value.reshape(-1, 8, value.shape[1]).sum(axis=0)


def core_kernel(
    init_ref,
    noise_ref,
    step_ref,
    length_ref,
    obs_ref,
    seen_ref,
    w_in_ref,
    b_in_ref,
    w_out_ref,
    b_out_ref,
    dec_ref,
    rate_ref,
    diff_ref,
    elbo_ref,
    grads_ref,
    small_ref,
    dec_grad_ref,
    cot_ref,
    x_ref,
    xt_ref,
    ut_ref,
    act_ref,
    pre_ref,
    scaled_ref,
    pick_ref,
    obs_wide_ref,
    dt_ref,
    root_ref,
    len_ref,
    state_ref,
    kl_ref,
    sum_b_in_ref,
    sum_b_out_ref,
    miss_ref,
):
    rows, width = init_ref.shape
    steps = noise_ref.shape[0]
    hidden = w_in_ref.shape[1]
    seen_count = obs_ref.shape[0]
    seen_width = dec_ref.shape[1]
    chunks = hidden // width

    def column(row):
        return jnp.broadcast_to(row, (rows, rows)).T

    dt_ref[...] = column(step_ref[...])
    root_ref[...] = jnp.sqrt(dt_ref[...])
    len_ref[...] = column(length_ref[...])
    for j in range(seen_count):
        obs_wide_ref[j] = column(obs_ref[j : j + 1, :])
    pick_ref[...] = jnp.zeros_like(pick_ref)
    kl_ref[...] = jnp.zeros_like(kl_ref)
    sum_b_in_ref[...] = jnp.zeros_like(sum_b_in_ref)
    sum_b_out_ref[...] = jnp.zeros_like(sum_b_out_ref)
    state_ref[...] = init_ref[...]
    x_ref[0] = init_ref[...].astype(BF16)

    def both(value):
        return jnp.concatenate([value] * (width // rows), axis=1)

    def forward(k, carry):
        x = x_ref[k]
        drift = jnp.broadcast_to(b_out_ref[...], (rows, width))
        for n in range(chunks):
            cols = slice(n * width, (n + 1) * width)
            act = jnp.tanh(dot(x, w_in_ref[:, cols]) + b_in_ref[:, cols]).astype(BF16)
            act_ref[n, pl.ds(k * rows, rows), :] = act
            drift = drift + dot(act, w_out_ref[cols, :])
        state = state_ref[...]
        inv = 1.0 / diff_ref[...]
        live = k < len_ref[...]
        factor = both(jnp.where(live, dt_ref[...], 0.0))
        root = both(jnp.where(live, root_ref[...], 0.0))
        residual = (drift + rate_ref[...] * state) * inv
        kl_ref[...] += factor * residual * residual
        scaled_ref[k] = residual * inv
        following = state + (
            factor * drift + diff_ref[...] * root * noise_ref[k].astype(F32)
        )
        state_ref[...] = following
        rounded = following.astype(BF16)
        x_ref[k + 1] = rounded
        xt_ref[:, pl.ds(pl.multiple_of(k * rows, rows), rows)] = x.T
        seen = dot(rounded, dec_ref[...])
        for j in range(seen_count):
            pick_ref[j] = jnp.where(obs_wide_ref[j] == k + 1, seen, pick_ref[j])
        return carry

    lax.fori_loop(0, steps, forward, 0)

    square = jnp.zeros((rows, seen_width), F32)
    for j in range(seen_count):
        misfit = pick_ref[j] - seen_ref[j].astype(F32)
        square = square + misfit * misfit
        pick_ref[j] = misfit.astype(BF16).astype(F32)
    loglik = -0.5 * jnp.sum(square.T, axis=0, keepdims=True)
    kl_half = kl_ref[:, :rows]
    for part in range(1, width // rows):
        kl_half = kl_half + kl_ref[:, part * rows : (part + 1) * rows]
    kl_row = 0.5 * jnp.sum(kl_half.T, axis=0, keepdims=True)
    divisor = (width * length_ref[...] + seen_width * seen_count).astype(F32)
    elbo_ref[...] = (loglik - kl_row) / divisor

    cot_ref[...] = jnp.zeros_like(cot_ref)

    def backward(index, carry):
        k = steps - 1 - index
        total = jnp.zeros((rows, seen_width), F32)
        for j in range(seen_count):
            total = total + jnp.where(obs_wide_ref[j] == k + 1, pick_ref[j], 0.0)
        high = total.astype(BF16)
        low = (total - high.astype(F32)).astype(BF16)
        miss_ref[pl.ds(k * rows, rows), :seen_width] = high
        miss_ref[pl.ds(k * rows, rows), seen_width:] = low
        obs_back = dot_nt(high, dec_ref[...]) + dot_nt(low, dec_ref[...])
        cot = cot_ref[...] + obs_back
        scaled = scaled_ref[k]
        factor = both(jnp.where(k < len_ref[...], dt_ref[...], 0.0))
        update = factor * (cot + scaled)
        rounded = update.astype(BF16)
        ut_ref[:, pl.ds(pl.multiple_of(k * rows, rows), rows)] = rounded.T
        sum_b_out_ref[...] += fold(update)
        cot = cot + factor * rate_ref[...] * scaled
        for n in range(chunks):
            cols = slice(n * width, (n + 1) * width)
            act = act_ref[n, pl.ds(k * rows, rows), :].astype(F32)
            pre = dot_nt(rounded, w_out_ref[cols, :]) * (1.0 - act * act)
            sum_b_in_ref[n] += fold(pre)
            pre_round = pre.astype(BF16)
            pre_ref[n, pl.ds(k * rows, rows), :] = pre_round
            cot = cot + dot_nt(pre_round, w_in_ref[:, cols])
        cot_ref[...] = cot
        return carry

    lax.fori_loop(0, steps, backward, 0)

    def gradients(n, carry):
        grads_ref[n, :width, :] = dot(xt_ref[...], pre_ref[n])
        grads_ref[n, width:, :] = dot(ut_ref[...], act_ref[n]).T
        return carry

    lax.fori_loop(0, chunks, gradients, 0)

    dec_grad = jnp.zeros((width, 2 * seen_width), F32)
    dec_grad = dec_grad + dot(xt_ref[:, rows:], miss_ref[: (steps - 1) * rows, :])
    last = lax.dot_general(
        x_ref[steps],
        miss_ref[(steps - 1) * rows :, :],
        (((0,), (0,)), ((), ())),
        preferred_element_type=F32,
    )
    dec_grad = dec_grad + last
    dec_grad_ref[...] = dec_grad[:, :seen_width] + dec_grad[:, seen_width:]
    for n in range(chunks):
        small_ref[n : n + 1, :] = jnp.sum(sum_b_in_ref[n], axis=0, keepdims=True)
    small_ref[chunks : chunks + 1, :] = jnp.sum(sum_b_out_ref[...], axis=0, keepdims=True)
    small_ref[chunks + 1 : chunks + 2, :rows] = loglik
    small_ref[chunks + 1 : chunks + 2, rows:] = kl_row
    small_ref[chunks + 2 :, :] = jnp.zeros((small_ref.shape[0] - chunks - 2, width), F32)


def core(init, noise, step, length, obs, seen, w_in, b_in, w_out, b_out, dec, rate, diff):
    rows, width = init.shape
    steps = noise.shape[0]
    hidden = w_in.shape[1]
    seen_count, seen_width = seen.shape[0], dec.shape[1]
    chunks = hidden // width
    vmem = pl.BlockSpec(memory_space=pltpu.VMEM)
    small_rows = -(-(chunks + 2) // 8) * 8
    out = [
        jax.ShapeDtypeStruct((1, rows), F32),
        jax.ShapeDtypeStruct((chunks, 2 * width, width), F32),
        jax.ShapeDtypeStruct((small_rows, width), F32),
        jax.ShapeDtypeStruct(dec.shape, F32),
        jax.ShapeDtypeStruct((rows, width), F32),
    ]
    scratch = [
        pltpu.VMEM((steps + 1, rows, width), BF16),
        pltpu.VMEM((width, steps * rows), BF16),
        pltpu.VMEM((width, steps * rows), BF16),
        pltpu.VMEM((chunks, steps * rows, width), BF16),
        pltpu.VMEM((chunks, steps * rows, width), BF16),
        pltpu.VMEM((steps, rows, width), F32),
        pltpu.VMEM((seen_count, rows, seen_width), F32),
        pltpu.VMEM((seen_count, rows, rows), jnp.int32),
        pltpu.VMEM((rows, rows), F32),
        pltpu.VMEM((rows, rows), F32),
        pltpu.VMEM((rows, rows), jnp.int32),
        pltpu.VMEM((rows, width), F32),
        pltpu.VMEM((rows, width), F32),
        pltpu.VMEM((chunks, 8, width), F32),
        pltpu.VMEM((8, width), F32),
        pltpu.VMEM((steps * rows, 2 * seen_width), BF16),
    ]
    return pl.pallas_call(
        core_kernel,
        out_shape=out,
        in_specs=[vmem] * 13,
        out_specs=[vmem] * 5,
        scratch_shapes=scratch,
        compiler_params=pltpu.CompilerParams(vmem_limit_bytes=60 * 1024 * 1024),
        name="sde",
    )(init, noise, step, length, obs, seen, w_in, b_in, w_out, b_out, dec, rate, diff)


def on_device(
    init_state,
    brownian,
    step_size,
    lengths,
    obs_steps,
    observed,
    w_in,
    b_in,
    w_out,
    b_out,
    decoder,
    prior_rate,
    diffusion,
):
    w_in_all, w_out_all, b_in_all = (
        lax.all_gather(w_in, "mp", axis=1, tiled=True),
        lax.all_gather(w_out, "mp", axis=0, tiled=True),
        lax.all_gather(b_in, "mp", axis=0, tiled=True),
    )
    rows, width = init_state.shape
    chunks = w_in_all.shape[1] // width
    elbo, grads, small, dec_grad, cot = core(
        init_state,
        brownian,
        step_size[None, :],
        lengths[None, :],
        obs_steps.T,
        observed.transpose(1, 0, 2),
        w_in_all,
        b_in_all.astype(F32)[None, :],
        w_out_all,
        b_out[None, :],
        decoder,
        prior_rate[None, :],
        diffusion[None, :],
    )
    total = rows * lax.axis_size("batch") * lax.axis_size("mp")
    mine = lax.axis_index("mp")
    grads = lax.psum_scatter(grads, "mp", scatter_dimension=0, tiled=True)[0]
    grads = lax.psum(grads, "batch") / total
    small, dec_grad = lax.psum((small, dec_grad), ("batch", "mp"))
    scores = jnp.stack([jnp.sum(small[chunks + 1, :rows]), jnp.sum(small[chunks + 1, rows:])])
    own_b_in = lax.dynamic_slice_in_dim(small, mine, 1, 0)[0]
    return (
        elbo[0],
        scores / total,
        grads[:width],
        own_b_in / total,
        grads[width:],
        small[chunks] / total,
        dec_grad / total,
        cot,
    )


def solution(mesh):
    both = ("batch", "mp")
    placed = (
        P(both, None),
        P(None, both, None),
        P(both),
        P(both),
        P(both, None),
        P(both, None, None),
        P(None, "mp"),
        P("mp"),
        P("mp", None),
        P(),
        P(),
        P(),
        P(),
    )
    return jax.shard_map(
        on_device,
        mesh=mesh,
        in_specs=placed,
        out_specs=(
            P(both),
            P(),
            P(None, "mp"),
            P("mp"),
            P("mp", None),
            P(),
            P(),
            P(both, None),
        ),
        check_vma=False,
    )
```

time: 931 us -> 307 us (0.33); the launches traced: 914 us -> 302 us
  matrix products: 310 us -> 0 us
  local copies, waits for them, and re-layouts: 237 us -> 3.21 us
  other arithmetic: 199 us -> 6.3 us
  waiting for transfers between devices: 90.5 us -> 168 us
  Pallas kernels: 0 us -> 48 us
    dot_general x196 -> x0, matrix products: 310 us -> none  [the longest x32 62.3 us: backward(): jnp.dot(pre_round, w_in_all.T, preferred_element_type=jnp.float32)]
    while x256 -> x0, local copies, waits for them, and re-layouts: 136 us -> none
    add x96 -> x0, other arithmetic: 77.8 us -> none  [the longest x32 39.1 us: backward(): sum_b_out = sum_b_out + jnp.sum(update, axis=0)]
    psum x1 -> x2, waiting for transfers between devices: 90.5 us -> 168 us  [the longest x1 94.9 us: on_device(): small, dec_grad = lax.psum((small, dec_grad), ('batch', 'mp'))]
    dynamic_slice x64 -> x0, local copies, waits for them, and re-layouts: 71.6 us -> none  [the longest x32 42.4 us: backward(): obs_here = lax.dynamic_index_in_dim(obs_back, step_index, 0, keepdims=False)]
    reduce_sum x66 -> x1, other arithmetic: 68.6 us -> 0.6 us  [on_device(): jnp.sum(small[chunks + 1, :rows])]
    pallas_call x0 -> x1, Pallas kernels: none -> 48 us  [core(): pl.pallas_call(core_kernel, out_shape=out, in_specs=[vmem] * 13, out_spec...]
    convert_element_type x34 -> x0, other arithmetic: 22 us -> none  [the longest x32 21.1 us: forward(): live_now = (step_index < lengths).astype(jnp.float32)]
  transfers between devices with their start and end apart: 1 -> 3, of which waited for: 1 -> 2; matrix products, arithmetic and copies ran while one was open for 0% -> 2% of each run, Pallas kernels for 0% -> 0%
where the time goes in v1:
time: 307 us; the launch traced here: 302 us
  waiting for transfers between devices  168 us (55%)
  blocking collectives  60.7 us (20%)
  Pallas kernels  48 us (16%)
  between operations  15.5 us (5%)
  other arithmetic  6.3 us (2%)
  local copies, waits for them, and re-layouts  3.21 us (1%)
    psum x1, waiting for transfers between devices, on_device(): small, dec_grad = lax.psum((small, dec_grad), ('batch', 'mp'))  94.9 us
    psum x1, waiting for transfers between devices, on_device(): grads = lax.psum(grads, 'batch') / total  73 us
    pallas_call x1, Pallas kernels, core(): pl.pallas_call(core_kernel, out_shape=out, in_specs=[vmem] * 13, out_spec...  48 us
    psum x1, blocking collectives, on_device(): small, dec_grad = lax.psum((small, dec_grad), ('batch', 'mp'))  38.1 us
    all_gather x1, blocking collectives, on_device(): lax.all_gather(w_in, 'mp', axis=1, tiled=True)  9.24 us
    all_gather x1, blocking collectives, on_device(): lax.all_gather(w_out, 'mp', axis=0, tiled=True)  8.27 us
  transfers between devices with their start and end apart: 3, of which 2 were waited for; matrix products, arithmetic and copies ran while one was open for 2% of the time, Pallas kernels for 0%

profile of v1, /device:TPU:25, one launch (start us, length us, event | category | flops | bytes accessed | tf_op | source)
XLA Modules:
  0.0 302.3 jit_solution(3498806840361989879)
XLA Ops:
  8.0 0.0 reduce-scatter.2.cloned.1.call-start
  8.0 1.7 copy.24
  9.7 9.2 %all_gather.9.w_in_ref = bf16[256,1024]{1,0:T(8,128)(2,1)} all-gather(bf16[256,256]{1,0:T(8,128)(2,1)} %param.19), channel_id=1, replica_groups=mesh['batch'=8,'mp'=4] {'mp'}, dimensions={1}, use_global_device_ids=true | all-gather | bytes 655360 | tf_op jit(solution)/shard_map/all_gather | solution.py:247
  19.0 0.7 reshape.21
  19.6 5.0 %all-gather = bf16[4,1,256]{2,1,0:T(2,128)(2,1)S(1)} all-gather(bf16[1,1,256]{2,1,0:T(2,128)(2,1)S(1)} %reshape.21), channel_id=1, replica_groups=mesh['batch'=8,'mp'=4] {'mp'}, dimensions={0}, use_global_device_ids=true | all-gather | bytes 2560 | tf_op jit(solution)/shard_map/all_gather | solution.py:249
  24.7 0.6 convert.1.b_in_ref
  25.3 8.3 %all_gather.11.w_out_ref = bf16[1024,256]{1,0:T(8,128)(2,1)} all-gather(bf16[256,256]{1,0:T(8,128)(2,1)} %param.21), channel_id=1, replica_groups=mesh['batch'=8,'mp'=4] {'mp'}, dimensions={0}, use_global_device_ids=true | all-gather | bytes 655360 | tf_op jit(solution)/shard_map/all_gather | solution.py:248
  33.6 48.0 %sde.1 = (f32[1,128]{1,0:T(1,128)}, f32[4,512,256]{2,1,0:T(8,128)}, f32[8,256]{1,0:T(8,128)}, f32[256,128]{1,0:T(8,128)}, f32[128,256]{1,0:T(8,128)}) custom-call(f32[128,256]{1,0:T(8,128)} %init_ref.1, bf16[32,128,256]{2,1,0:T(8,128)(2,1)} %noise_ref.1, f32[1,128]{1,0:T(1,128)} %bitcast.26, s32[1,128]{1,0:T(1,128)} %bitcast.27, s32[8,128]{1,0:T(8,128)} %bitcast.20, ...), custom_call_target="tpu_custom_call" | custom-call | tf_op jit(solution)/shard_map/sde/pallas_call | solution.py:220
  81.6 0.0 copy-start
  81.6 0.0 reduce-scatter.2.cloned.1.call-update
  81.6 0.0 all-reduce.5.cloned.1.call-start
  81.6 0.5 all-reduce.5.cloned.1.call-update
  82.2 0.0 all-reduce.3.cloned.1.call-start
  82.2 0.0 copy-done
  82.3 38.1 %psum.21 = f32[8,256]{1,0:T(8,128)S(1)} all-reduce(f32[8,256]{1,0:T(8,128)S(1)} %copy-done), channel_id=1, replica_groups=mesh['batch'=8,'mp'=4] {'batch','mp'}, use_global_device_ids=true, to_apply=%region_0.0 | all-reduce | flops 2048 | bytes 16384 | tf_op jit(solution)/shard_map/psum | solution.py:272
  120.4 0.6 slice_reduce_fusion.1
  121.0 0.0 reduce-scatter.2.cloned.1.call-done
  121.0 0.0 all-reduce.3.cloned.1.call-update
  121.0 1.9 maximum_multiply_fusion
  122.9 0.6 slice_multiply_fusion
  123.5 94.9 %all-reduce.5.cloned.1.call-done = f32[256,128]{1,0:T(8,128)} async-done(((f32[256,128]{1,0:T(8,128)}), f32[256,128]{1,0:T(8,128)}) %all-reduce.5.cloned.1.call-update) | async-done | bytes 131088 | tf_op jit(solution)/shard_map/psum | solution.py:272
  218.4 1.6 broadcast_multiply_fusion.1
  219.9 73.0 %all-reduce.3.cloned.1.call-done = f32[512,256]{1,0:T(8,128)} async-done(((f32[512,256]{1,0:T(8,128)}), f32[512,256]{1,0:T(8,128)}) %all-reduce.3.cloned.1.call-update) | async-done | bytes 524304 | tf_op jit(solution)/shard_map/psum | solution.py:271
  292.9 1.1 broadcast_multiply_fusion
  294.0 0.8 fusion
Async XLA Ops:
  8.0 113.0 %reduce-scatter.2.cloned.1.call-start = ((), (), s32[]{:S(2)}) async-start(), calls=%async_computation.1 | async-start | bytes 2621440 | tf_op jit(solution)/shard_map/reduce_scatter | solution.py:270
  81.6 0.7 copy-start
  81.6 136.8 %all-reduce.5.cloned.1.call-start = ((), (), s32[]{:S(2)}) async-start(), calls=%async_computation.3 | async-start | bytes 262144 | tf_op jit(solution)/shard_map/psum | solution.py:272
  82.2 210.8 %all-reduce.3.cloned.1.call-start = ((), (), s32[]{:S(2)}) async-start(), calls=%async_computation.2 | async-start | bytes 1048576 | tf_op jit(solution)/shard_map/psum | solution.py:271
Sparse Core Ops, SparseCore 0:
  81.7 31.5 reduce-scatter.1
Sparse Core Ops, SparseCore 1:
  88.2 130.1 all-reduce.4
  221.7 71.2 all-reduce.2

commit v2 on v1

--- a/solution.py
+++ b/solution.py
@@ -38,8 +38,6 @@
     diff_ref,
     elbo_ref,
     grads_ref,
-    small_ref,
-    dec_grad_ref,
     cot_ref,
     x_ref,
     xt_ref,
@@ -60,10 +58,9 @@
 ):
     rows, width = init_ref.shape
     steps = noise_ref.shape[0]
-    hidden = w_in_ref.shape[1]
     seen_count = obs_ref.shape[0]
     seen_width = dec_ref.shape[1]
-    chunks = hidden // width
+    chunks = w_in_ref.shape[0]
 
     def column(row):
         return jnp.broadcast_to(row, (rows, rows)).T
@@ -87,10 +84,9 @@
         x = x_ref[k]
         drift = jnp.broadcast_to(b_out_ref[...], (rows, width))
         for n in range(chunks):
-            cols = slice(n * width, (n + 1) * width)
-            act = jnp.tanh(dot(x, w_in_ref[:, cols]) + b_in_ref[:, cols]).astype(BF16)
+            act = jnp.tanh(dot(x, w_in_ref[n]) + b_in_ref[n, :1, :]).astype(BF16)
             act_ref[n, pl.ds(k * rows, rows), :] = act
-            drift = drift + dot(act, w_out_ref[cols, :])
+            drift = drift + dot(act, w_out_ref[n])
         state = state_ref[...]
         inv = 1.0 / diff_ref[...]
         live = k < len_ref[...]
@@ -147,13 +143,12 @@
         sum_b_out_ref[...] += fold(update)
         cot = cot + factor * rate_ref[...] * scaled
         for n in range(chunks):
-            cols = slice(n * width, (n + 1) * width)
             act = act_ref[n, pl.ds(k * rows, rows), :].astype(F32)
-            pre = dot_nt(rounded, w_out_ref[cols, :]) * (1.0 - act * act)
+            pre = dot_nt(rounded, w_out_ref[n]) * (1.0 - act * act)
             sum_b_in_ref[n] += fold(pre)
             pre_round = pre.astype(BF16)
             pre_ref[n, pl.ds(k * rows, rows), :] = pre_round
-            cot = cot + dot_nt(pre_round, w_in_ref[:, cols])
+            cot = cot + dot_nt(pre_round, w_in_ref[n])
         cot_ref[...] = cot
         return carry
 
@@ -161,7 +156,7 @@
 
     def gradients(n, carry):
         grads_ref[n, :width, :] = dot(xt_ref[...], pre_ref[n])
-        grads_ref[n, width:, :] = dot(ut_ref[...], act_ref[n]).T
+        grads_ref[n, width : 2 * width, :] = dot(ut_ref[...], act_ref[n]).T
         return carry
 
     lax.fori_loop(0, chunks, gradients, 0)
@@ -175,28 +170,35 @@
         preferred_element_type=F32,
     )
     dec_grad = dec_grad + last
-    dec_grad_ref[...] = dec_grad[:, :seen_width] + dec_grad[:, seen_width:]
+    dec_grad = dec_grad[:, :seen_width] + dec_grad[:, seen_width:]
+    lanes = width // seen_width
+    share = width // chunks
+    tail = 2 * width
+    line = tail + share // lanes
     for n in range(chunks):
-        small_ref[n : n + 1, :] = jnp.sum(sum_b_in_ref[n], axis=0, keepdims=True)
-    small_ref[chunks : chunks + 1, :] = jnp.sum(sum_b_out_ref[...], axis=0, keepdims=True)
-    small_ref[chunks + 1 : chunks + 2, :rows] = loglik
-    small_ref[chunks + 1 : chunks + 2, rows:] = kl_row
-    small_ref[chunks + 2 :, :] = jnp.zeros((small_ref.shape[0] - chunks - 2, width), F32)
-
-
-def core(init, noise, step, length, obs, seen, w_in, b_in, w_out, b_out, dec, rate, diff):
+        pieces = [
+            dec_grad[n * share + m * share // lanes : n * share + (m + 1) * share // lanes, :]
+            for m in range(lanes)
+        ]
+        grads_ref[n, tail:line, :] = jnp.concatenate(pieces, axis=1)
+        grads_ref[n, line:, :] = jnp.zeros((grads_ref.shape[1] - line, width), F32)
+        grads_ref[n, line : line + 1, :] = jnp.sum(sum_b_in_ref[n], axis=0, keepdims=True)
+        grads_ref[n, line + 1 : line + 2, :] = jnp.sum(
+            sum_b_out_ref[...], axis=0, keepdims=True
+        )
+        grads_ref[n, line + 2 : line + 3, :rows] = loglik
+        grads_ref[n, line + 2 : line + 3, rows : 2 * rows] = kl_row
+
+
+def core(grad_rows, init, noise, step, length, obs, seen, w_in, b_in, w_out, b_out, dec, rate, diff):
     rows, width = init.shape
     steps = noise.shape[0]
-    hidden = w_in.shape[1]
     seen_count, seen_width = seen.shape[0], dec.shape[1]
-    chunks = hidden // width
+    chunks = w_in.shape[0]
     vmem = pl.BlockSpec(memory_space=pltpu.VMEM)
-    small_rows = -(-(chunks + 2) // 8) * 8
     out = [
         jax.ShapeDtypeStruct((1, rows), F32),
-        jax.ShapeDtypeStruct((chunks, 2 * width, width), F32),
-        jax.ShapeDtypeStruct((small_rows, width), F32),
-        jax.ShapeDtypeStruct(dec.shape, F32),
+        jax.ShapeDtypeStruct((chunks, grad_rows, width), F32),
         jax.ShapeDtypeStruct((rows, width), F32),
     ]
     scratch = [
@@ -221,11 +223,282 @@
         core_kernel,
         out_shape=out,
         in_specs=[vmem] * 13,
-        out_specs=[vmem] * 5,
+        out_specs=[vmem] * 3,
         scratch_shapes=scratch,
         compiler_params=pltpu.CompilerParams(vmem_limit_bytes=60 * 1024 * 1024),
         name="sde",
     )(init, noise, step, length, obs, seen, w_in, b_in, w_out, b_out, dec, rate, diff)
+
+
+def send(source, target, send_sem, recv_sem, peer):
+    return pltpu.make_async_remote_copy(
+        src_ref=source,
+        dst_ref=target,
+        send_sem=send_sem,
+        recv_sem=recv_sem,
+        device_id=peer,
+        device_id_type=pl.DeviceIdType.MESH,
+    )
+
+
+def greet(peers):
+    barrier = pltpu.get_barrier_semaphore()
+    for peer in peers:
+        pl.semaphore_signal(barrier, inc=1, device_id=peer, device_id_type=pl.DeviceIdType.MESH)
+    pl.semaphore_wait(barrier, len(peers))
+
+
+def mp_places():
+    mine = lax.axis_index("mp")
+    chip, unit = mine // 2, mine % 2
+    sibling = chip * 2 + (1 - unit)
+    across = (1 - chip) * 2 + unit
+    diagonal = (1 - chip) * 2 + (1 - unit)
+    return mine, sibling, across, diagonal
+
+
+def gather_kernel(w_in_ref, w_out_ref, b_in_ref, all_in_ref, all_out_ref, all_b_ref, bias_ref, send_sem, recv_sem):
+    mine, sibling, across, diagonal = mp_places()
+    batch = lax.axis_index("batch")
+    to_across, to_sibling = (batch, across), (batch, sibling)
+    bias_ref[...] = jnp.broadcast_to(b_in_ref[...].astype(F32), bias_ref.shape)
+    greet([to_across, to_sibling])
+    pairs = ((w_in_ref, all_in_ref), (w_out_ref, all_out_ref), (bias_ref, all_b_ref))
+    far, near, relayed = [], [], []
+    for i, (own, whole) in enumerate(pairs):
+        copy = send(own, whole.at[mine], send_sem.at[0, i], recv_sem.at[0, i], to_across)
+        copy.start()
+        far.append(copy)
+    for i, (own, whole) in enumerate(pairs):
+        copy = send(own, whole.at[mine], send_sem.at[1, i], recv_sem.at[1, i], to_sibling)
+        copy.start()
+        near.append(copy)
+    for own, whole in pairs:
+        whole[mine] = own[...]
+    for i, (own, whole) in enumerate(pairs):
+        far[i].wait_recv()
+        copy = send(
+            whole.at[across], whole.at[across], send_sem.at[2, i], recv_sem.at[2, i], to_sibling
+        )
+        copy.start()
+        relayed.append(copy)
+    for copy in far:
+        copy.wait_send()
+    for copy in near + relayed:
+        copy.wait()
+
+
+def gather(w_in, w_out, b_in):
+    count = lax.axis_size("mp")
+    vmem = pl.BlockSpec(memory_space=pltpu.VMEM)
+    return pl.pallas_call(
+        gather_kernel,
+        out_shape=[
+            jax.ShapeDtypeStruct((count,) + w_in.shape, BF16),
+            jax.ShapeDtypeStruct((count,) + w_out.shape, BF16),
+            jax.ShapeDtypeStruct((count, 8, b_in.shape[1]), F32),
+        ],
+        in_specs=[vmem] * 3,
+        out_specs=[vmem] * 3,
+        scratch_shapes=[
+            pltpu.VMEM((8, b_in.shape[1]), F32),
+            pltpu.SemaphoreType.DMA((3, 3)),
+            pltpu.SemaphoreType.DMA((3, 3)),
+        ],
+        compiler_params=pltpu.CompilerParams(
+            collective_id=0, has_side_effects=True, vmem_limit_bytes=16 * 1024 * 1024
+        ),
+        name="gather_weights",
+    )(w_in, w_out, b_in)
+
+
+def reduce_kernel(
+    members,
+    total,
+    share,
+    grads_ref,
+    w_in_ref,
+    w_out_ref,
+    b_in_ref,
+    b_out_ref,
+    dec_ref,
+    scores_ref,
+    near_ref,
+    far_w_ref,
+    far_t_ref,
+    got_w_ref,
+    got_t_ref,
+    full_ref,
+    parts_ref,
+    done_ref,
+    decs_ref,
+    near_send,
+    near_recv,
+    far_send,
+    far_recv,
+    rs_send,
+    rs_recv,
+    ag_send,
+    ag_recv,
+    dec_send,
+    dec_recv,
+):
+    mine, sibling, across, diagonal = mp_places()
+    batch = lax.axis_index("batch")
+    width = grads_ref.shape[2]
+    weight_rows = 2 * width
+    piece = grads_ref.shape[1] // members
+    others = [(lax.rem(batch + d, members), mine) for d in range(1, members)]
+    group = [(batch, sibling), (batch, across), (batch, diagonal)]
+    greet(group + others)
+    near = []
+    for i, quarter in enumerate((diagonal, sibling)):
+        copy = send(
+            grads_ref.at[quarter], near_ref.at[i], near_send.at[i], near_recv.at[i], group[0]
+        )
+        copy.start()
+        near.append(copy)
+    near[0].wait_recv()
+    far_w_ref[...] = (
+        grads_ref[across, :weight_rows, :] + near_ref[0, :weight_rows, :]
+    ).astype(BF16)
+    far_t_ref[...] = grads_ref[across, weight_rows:, :] + near_ref[0, weight_rows:, :]
+    far = [
+        send(far_w_ref, got_w_ref, far_send.at[0], far_recv.at[0], group[1]),
+        send(far_t_ref, got_t_ref, far_send.at[1], far_recv.at[1], group[1]),
+    ]
+    for copy in far:
+        copy.start()
+    near[1].wait_recv()
+    full_ref[...] = grads_ref[mine] + near_ref[1]
+    far[0].wait_recv()
+    full_ref[:weight_rows, :] += got_w_ref[...].astype(F32)
+    far[1].wait_recv()
+    full_ref[weight_rows:, :] += got_t_ref[...]
+    scatter = []
+    for d in range(1, members):
+        target = lax.rem(batch + d, members)
+        copy = send(
+            full_ref.at[pl.ds(pl.multiple_of(target * piece, 8), piece), :],
+            parts_ref.at[d - 1],
+            rs_send.at[d - 1],
+            rs_recv.at[d - 1],
+            others[d - 1],
+        )
+        copy.start()
+        scatter.append(copy)
+    here = pl.ds(pl.multiple_of(batch * piece, 8), piece)
+    value = full_ref[here, :]
+    for d in range(1, members):
+        scatter[d - 1].wait_recv()
+        value = value + parts_ref[d - 1]
+    done_ref[here, :] = value / total
+    spread = []
+    for d in range(1, members):
+        copy = send(
+            done_ref.at[here, :],
+            done_ref.at[here, :],
+            ag_send.at[d - 1],
+            ag_recv.at[d - 1],
+            others[d - 1],
+        )
+        copy.start()
+        spread.append(copy)
+    for copy in near + far + scatter:
+        copy.wait_send()
+    for d in range(1, members):
+        origin = lax.rem(batch + members - d, members)
+        there = pl.ds(pl.multiple_of(origin * piece, 8), piece)
+        send(
+            done_ref.at[there, :],
+            done_ref.at[there, :],
+            ag_send.at[d - 1],
+            ag_recv.at[d - 1],
+            others[d - 1],
+        ).wait_recv()
+    dec_rows = decs_ref.shape[1]
+    line = weight_rows + dec_rows
+    exchange = []
+    for i in range(3):
+        copy = send(
+            done_ref.at[pl.ds(weight_rows, dec_rows), :],
+            decs_ref.at[mine],
+            dec_send.at[i],
+            dec_recv.at[i],
+            group[i],
+        )
+        copy.start()
+        exchange.append(copy)
+    w_in_ref[...] = done_ref[:width, :]
+    w_out_ref[...] = done_ref[width:weight_rows, :]
+    decs_ref[mine] = done_ref[weight_rows:line, :]
+    b_in_ref[...] = done_ref[line : line + 1, :]
+    b_out_ref[...] = done_ref[line + 1 : line + 2, :]
+    half = share
+    scores_ref[:, 0:1] = jnp.sum(done_ref[line + 2 : line + 3, :half], axis=1, keepdims=True)
+    scores_ref[:, 1:2] = jnp.sum(
+        done_ref[line + 2 : line + 3, half : 2 * half], axis=1, keepdims=True
+    )
+    for copy in spread:
+        copy.wait_send()
+    for i, origin in enumerate((sibling, across, diagonal)):
+        exchange[i].wait_send()
+        send(
+            decs_ref.at[origin], decs_ref.at[origin], dec_send.at[i], dec_recv.at[i], group[i]
+        ).wait_recv()
+    seen_width = dec_ref.shape[1]
+    for n in range(decs_ref.shape[0]):
+        for m in range(width // seen_width):
+            start = (n * (width // seen_width) + m) * dec_rows
+            dec_ref[start : start + dec_rows, :] = decs_ref[
+                n, :, m * seen_width : (m + 1) * seen_width
+            ]
+
+
+def reduce_all(grads, rows, seen_width):
+    quarters, grad_rows, width = grads.shape
+    members = lax.axis_size("batch")
+    total = rows * members * lax.axis_size("mp")
+    dec_rows = width // quarters // (width // seen_width)
+    tail_rows = grad_rows - 2 * width
+    piece = grad_rows // members
+    vmem = pl.BlockSpec(memory_space=pltpu.VMEM)
+    sems = []
+    for count in (2, 2, members - 1, members - 1, 3):
+        sems += [pltpu.SemaphoreType.DMA((count,))] * 2
+
+    def body(*refs):
+        reduce_kernel(members, total, rows, *refs)
+
+    return pl.pallas_call(
+        body,
+        out_shape=[
+            jax.ShapeDtypeStruct((width, width), F32),
+            jax.ShapeDtypeStruct((width, width), F32),
+            jax.ShapeDtypeStruct((1, width), F32),
+            jax.ShapeDtypeStruct((1, width), F32),
+            jax.ShapeDtypeStruct((width, seen_width), F32),
+            jax.ShapeDtypeStruct((1, 2), F32),
+        ],
+        in_specs=[vmem],
+        out_specs=[vmem] * 6,
+        scratch_shapes=[
+            pltpu.VMEM((2, grad_rows, width), F32),
+            pltpu.VMEM((2 * width, width), BF16),
+            pltpu.VMEM((tail_rows, width), F32),
+            pltpu.VMEM((2 * width, width), BF16),
+            pltpu.VMEM((tail_rows, width), F32),
+            pltpu.VMEM((grad_rows, width), F32),
+            pltpu.VMEM((members - 1, piece, width), F32),
+            pltpu.VMEM((grad_rows, width), F32),
+            pltpu.VMEM((quarters, dec_rows, width), F32),
+        ]
+        + sems,
+        compiler_params=pltpu.CompilerParams(
+            collective_id=1, has_side_effects=True, vmem_limit_bytes=32 * 1024 * 1024
+        ),
+        name="reduce_grads",
+    )(grads)
 
 
 def on_device(
@@ -243,14 +516,13 @@
     prior_rate,
     diffusion,
 ):
-    w_in_all, w_out_all, b_in_all = (
-        lax.all_gather(w_in, "mp", axis=1, tiled=True),
-        lax.all_gather(w_out, "mp", axis=0, tiled=True),
-        lax.all_gather(b_in, "mp", axis=0, tiled=True),
-    )
     rows, width = init_state.shape
-    chunks = w_in_all.shape[1] // width
-    elbo, grads, small, dec_grad, cot = core(
+    seen_width = decoder.shape[1]
+    w_in_all, w_out_all, b_in_all = gather(w_in, w_out, b_in[None, :])
+    unit = 8 * lax.axis_size("batch")
+    need = 2 * width + width // lax.axis_size("mp") * seen_width // width + 3
+    elbo, grads, cot = core(
+        -(-need // unit) * unit,
         init_state,
         brownian,
         step_size[None, :],
@@ -258,28 +530,24 @@
         obs_steps.T,
         observed.transpose(1, 0, 2),
         w_in_all,
-        b_in_all.astype(F32)[None, :],
+        b_in_all,
         w_out_all,
         b_out[None, :],
         decoder,
         prior_rate[None, :],
         diffusion[None, :],
     )
-    total = rows * lax.axis_size("batch") * lax.axis_size("mp")
-    mine = lax.axis_index("mp")
-    grads = lax.psum_scatter(grads, "mp", scatter_dimension=0, tiled=True)[0]
-    grads = lax.psum(grads, "batch") / total
-    small, dec_grad = lax.psum((small, dec_grad), ("batch", "mp"))
-    scores = jnp.stack([jnp.sum(small[chunks + 1, :rows]), jnp.sum(small[chunks + 1, rows:])])
-    own_b_in = lax.dynamic_slice_in_dim(small, mine, 1, 0)[0]
+    own_w_in, own_w_out, own_b_in, b_out_grad, dec_grad, scores = reduce_all(
+        grads, rows, seen_width
+    )
     return (
         elbo[0],
-        scores / total,
-        grads[:width],
-        own_b_in / total,
-        grads[width:],
-        small[chunks] / total,
-        dec_grad / total,
+        scores[0],
+        own_w_in,
+        own_b_in[0],
+        own_w_out,
+        b_out_grad[0],
+        dec_grad,
         cot,
     )
 

time: 307 us -> 118 us (0.38); the launches traced: 302 us -> 117 us
  waiting for transfers between devices: 168 us -> 0 us
  blocking collectives: 60.7 us -> 0 us
  Pallas kernels: 48 us -> 105 us
  between operations: 15.5 us -> 0.67 us
  local copies, waits for them, and re-layouts: 3.21 us -> 11.7 us
  other arithmetic: 6.3 us -> 0 us
    psum x2 -> x0, waiting for transfers between devices: 168 us -> none  [the longest x1 94.9 us: on_device(): small, dec_grad = lax.psum((small, dec_grad), ('batch', 'mp'))]
    pallas_call x0 -> x2, Pallas kernels: none -> 56.1 us  [the longest x1 45.8 us: reduce_all(): pl.pallas_call(body, out_shape=[jax.ShapeDtypeStruct((width, width), F32)...]
    psum x1 -> x0, blocking collectives: 38.1 us -> none  [on_device(): small, dec_grad = lax.psum((small, dec_grad), ('batch', 'mp'))]
    all_gather x3 -> x0, blocking collectives: 22.6 us -> none  [the longest x1 9.24 us: on_device(): lax.all_gather(w_in, 'mp', axis=1, tiled=True)]
    unnamed x4 -> x19, local copies, waits for them, and re-layouts: 2.39 us -> 11.1 us
    div x4 -> x0, other arithmetic: 5.1 us -> none  [the longest x1 1.88 us: on_device(): scores / total]
  transfers between devices with their start and end apart: 3 -> 0, of which waited for: 2 -> 0; matrix products, arithmetic and copies ran while one was open for 2% -> 0% of each run, Pallas kernels for 0% -> 0%
where the time goes in v2:
time: 118 us; the launch traced here: 117 us
  Pallas kernels  105 us (89%)
  local copies, waits for them, and re-layouts  11.7 us (10%)
    pallas_call x1, Pallas kernels, core(): pl.pallas_call(core_kernel, out_shape=out, in_specs=[vmem] * 13, out_spec...  48.5 us
    pallas_call x1, Pallas kernels, reduce_all(): pl.pallas_call(body, out_shape=[jax.ShapeDtypeStruct((width, width), F32)...  45.8 us
    unnamed x19, local copies, waits for them, and re-layouts  11.1 us
    pallas_call x1, Pallas kernels, gather(): pl.pallas_call(gather_kernel, out_shape=[jax.ShapeDtypeStruct((count,) +...  10.2 us

profile of v2, /device:TPU:25, one launch (start us, length us, event | category | flops | bytes accessed | tf_op | source)
XLA Modules:
  0.0 117.0 jit_solution(14612468237357645251)
XLA Ops:
  0.6 0.7 broadcast_in_dim.20.b_in_ref
  1.3 1.7 %copy.23 = bf16[128,8,128]{2,0,1:T(8,128)(2,1)} copy(bf16[128,8,128]{2,1,0:T(8,128)(2,1)} %param.18) | data formatting | bytes 524288 | tf_op args[5]
  3.0 0.0 copy-start.3
  3.0 0.9 copy-done.3
  3.9 0.0 copy-start.4
  3.9 0.9 copy-done.4
  4.8 10.2 %gather_weights.1 = (bf16[4,256,256]{2,1,0:T(8,128)(2,1)S(1)}, bf16[4,256,256]{2,1,0:T(8,128)(2,1)S(1)}, f32[4,8,256]{2,1,0:T(8,128)S(1)}) custom-call(bf16[256,256]{1,0:T(8,128)(2,1)S(1)} %copy-done.3, bf16[256,256]{1,0:T(8,128)(2,1)S(1)} %copy-done.4, bf16[1,256]{1,0:T(2,128)(2,1)S(1)} %broadcast_in_dim.20.b_in_ref), custom_call_target="tpu_custom_call" | custom-call | tf_op jit(solution)/shard_map/gather_weights/pallas_call | solution.py:294
  15.0 0.0 copy-start.1
  15.0 0.8 copy-done.1
  15.8 0.0 copy-start.2
  15.8 0.8 copy-done.2
  16.6 0.0 copy-start.5
  16.6 0.6 copy-done.5
  17.3 48.5 %sde.1 = (f32[1,128]{1,0:T(1,128)}, f32[4,576,256]{2,1,0:T(8,128)}, f32[128,256]{1,0:T(8,128)}) custom-call(f32[128,256]{1,0:T(8,128)} %init_ref.1, bf16[32,128,256]{2,1,0:T(8,128)(2,1)} %noise_ref.1, f32[1,128]{1,0:T(1,128)} %bitcast.21, s32[1,128]{1,0:T(1,128)} %bitcast.22, s32[8,128]{1,0:T(8,128)} %bitcast.17, bf16[8,128,128]{2,1,0:T(8,128)(2,1)} %bitcast.16, ...), custom_call_target="tpu_custom_call" | custom-call | tf_op jit(solution)/shard_map/sde/pallas_call | solution.py:222
  65.8 0.0 copy-start
  65.8 1.7 %copy-done = f32[4,576,256]{2,1,0:T(8,128)S(1)} copy-done((f32[4,576,256]{2,1,0:T(8,128)S(1)}, f32[4,576,256]{2,1,0:T(8,128)}, u32[]{:S(2)}) %copy-start) | copy-done | bytes 2359320
  67.5 45.8 %reduce_grads.1 = (f32[256,256]{1,0:T(8,128)S(1)}, f32[256,256]{1,0:T(8,128)S(1)}, f32[1,256]{1,0:T(1,128)S(1)}, f32[1,256]{1,0:T(1,128)S(1)}, f32[256,128]{1,0:T(8,128)S(1)}, /*index=5*/f32[1,2]{1,0:T(1,128)S(1)}) custom-call(f32[4,576,256]{2,1,0:T(8,128)S(1)} %copy-done), custom_call_target="tpu_custom_call" | custom-call | tf_op jit(solution)/shard_map/reduce_grads/pallas_call | solution.py:473
  113.3 0.5 copy.30
  113.8 0.7 copy.31
  114.5 0.6 copy.32
  115.1 0.7 copy.33
  115.8 0.6 copy.34
  116.4 0.7 copy.35
Async XLA Ops:
  3.0 0.9 copy-start.3
  3.9 0.9 copy-start.4
  15.0 0.8 copy-start.1
  15.8 0.8 copy-start.2
  16.6 0.6 copy-start.5
  65.8 1.7 %copy-start = (f32[4,576,256]{2,1,0:T(8,128)S(1)}, f32[4,576,256]{2,1,0:T(8,128)}, u32[]{:S(2)}) copy-start(f32[4,576,256]{2,1,0:T(8,128)} %get-tuple-element.24.refs_0_) | copy-start | bytes 7077892

commit v3 on v2

--- a/solution.py
+++ b/solution.py
@@ -55,6 +55,7 @@
     sum_b_in_ref,
     sum_b_out_ref,
     miss_ref,
+    target_ref,
 ):
     rows, width = init_ref.shape
     steps = noise_ref.shape[0]
@@ -70,6 +71,7 @@
     len_ref[...] = column(length_ref[...])
     for j in range(seen_count):
         obs_wide_ref[j] = column(obs_ref[j : j + 1, :])
+    target_ref[...] = seen_ref[...].astype(F32).reshape(target_ref.shape)
     pick_ref[...] = jnp.zeros_like(pick_ref)
     kl_ref[...] = jnp.zeros_like(kl_ref)
     sum_b_in_ref[...] = jnp.zeros_like(sum_b_in_ref)
@@ -111,7 +113,7 @@
 
     square = jnp.zeros((rows, seen_width), F32)
     for j in range(seen_count):
-        misfit = pick_ref[j] - seen_ref[j].astype(F32)
+        misfit = pick_ref[j] - target_ref[pl.ds(j, rows, stride=seen_count), :]
         square = square + misfit * misfit
         pick_ref[j] = misfit.astype(BF16).astype(F32)
     loglik = -0.5 * jnp.sum(square.T, axis=0, keepdims=True)
@@ -193,7 +195,7 @@
 def core(grad_rows, init, noise, step, length, obs, seen, w_in, b_in, w_out, b_out, dec, rate, diff):
     rows, width = init.shape
     steps = noise.shape[0]
-    seen_count, seen_width = seen.shape[0], dec.shape[1]
+    seen_count, seen_width = seen.shape[1], dec.shape[1]
     chunks = w_in.shape[0]
     vmem = pl.BlockSpec(memory_space=pltpu.VMEM)
     out = [
@@ -218,6 +220,7 @@
         pltpu.VMEM((chunks, 8, width), F32),
         pltpu.VMEM((8, width), F32),
         pltpu.VMEM((steps * rows, 2 * seen_width), BF16),
+        pltpu.VMEM((rows * seen_count, seen_width), F32),
     ]
     return pl.pallas_call(
         core_kernel,
@@ -225,7 +228,12 @@
         in_specs=[vmem] * 13,
         out_specs=[vmem] * 3,
         scratch_shapes=scratch,
-        compiler_params=pltpu.CompilerParams(vmem_limit_bytes=60 * 1024 * 1024),
+        compiler_params=pltpu.CompilerParams(vmem_limit_bytes=44 * 1024 * 1024),
+        cost_estimate=pl.CostEstimate(
+            flops=12 * steps * rows * width * width * chunks,
+            bytes_accessed=8 << 20,
+            transcendentals=steps * rows * width * chunks,
+        ),
         name="sde",
     )(init, noise, step, length, obs, seen, w_in, b_in, w_out, b_out, dec, rate, diff)
 
@@ -306,8 +314,9 @@
             pltpu.SemaphoreType.DMA((3, 3)),
         ],
         compiler_params=pltpu.CompilerParams(
-            collective_id=0, has_side_effects=True, vmem_limit_bytes=16 * 1024 * 1024
+            collective_id=0, has_side_effects=True, vmem_limit_bytes=8 * 1024 * 1024
         ),
+        cost_estimate=pl.CostEstimate(flops=0, bytes_accessed=32 << 20, transcendentals=0),
         name="gather_weights",
     )(w_in, w_out, b_in)
 
@@ -329,6 +338,7 @@
     got_w_ref,
     got_t_ref,
     full_ref,
+    round_ref,
     parts_ref,
     done_ref,
     decs_ref,
@@ -375,11 +385,13 @@
     full_ref[:weight_rows, :] += got_w_ref[...].astype(F32)
     far[1].wait_recv()
     full_ref[weight_rows:, :] += got_t_ref[...]
+    for p in range(members):
+        round_ref[p] = full_ref[p * piece : (p + 1) * piece, :].astype(BF16)
     scatter = []
     for d in range(1, members):
         target = lax.rem(batch + d, members)
         copy = send(
-            full_ref.at[pl.ds(pl.multiple_of(target * piece, 8), piece), :],
+            round_ref.at[target],
             parts_ref.at[d - 1],
             rs_send.at[d - 1],
             rs_recv.at[d - 1],
@@ -391,7 +403,7 @@
     value = full_ref[here, :]
     for d in range(1, members):
         scatter[d - 1].wait_recv()
-        value = value + parts_ref[d - 1]
+        value = value + parts_ref[d - 1].astype(F32)
     done_ref[here, :] = value / total
     spread = []
     for d in range(1, members):
@@ -489,13 +501,14 @@
             pltpu.VMEM((2 * width, width), BF16),
             pltpu.VMEM((tail_rows, width), F32),
             pltpu.VMEM((grad_rows, width), F32),
-            pltpu.VMEM((members - 1, piece, width), F32),
+            pltpu.VMEM((members, piece, width), BF16),
+            pltpu.VMEM((members - 1, piece, width), BF16),
             pltpu.VMEM((grad_rows, width), F32),
             pltpu.VMEM((quarters, dec_rows, width), F32),
         ]
         + sems,
         compiler_params=pltpu.CompilerParams(
-            collective_id=1, has_side_effects=True, vmem_limit_bytes=32 * 1024 * 1024
+            collective_id=1, has_side_effects=True, vmem_limit_bytes=16 * 1024 * 1024
         ),
         name="reduce_grads",
     )(grads)
@@ -528,7 +541,7 @@
         step_size[None, :],
         lengths[None, :],
         obs_steps.T,
-        observed.transpose(1, 0, 2),
+        observed,
         w_in_all,
         b_in_all,
         w_out_all,

time: 118 us -> 110 us (0.932)
  Pallas kernels: 105 us -> 94.7 us
  local copies, waits for them, and re-layouts: 11.7 us -> 14.5 us
    pallas_call x1, Pallas kernels: 45.8 us -> 39.3 us  [reduce_all(): pl.pallas_call(body, out_shape=[jax.ShapeDtypeStruct((width, width), F32)...]
    pallas_call x1, Pallas kernels: 48.5 us -> 45.2 us  [core(): pl.pallas_call(core_kernel, out_shape=out, in_specs=[vmem] * 13, out_spec...]
    unnamed x19 -> x30, local copies, waits for them, and re-layouts: 11.1 us -> 13.8 us
where the time goes in v3:
time: 110 us
  Pallas kernels  94.7 us (86%)
  local copies, waits for them, and re-layouts  14.5 us (13%)
    pallas_call x1, Pallas kernels, core(): pl.pallas_call(core_kernel, out_shape=out, in_specs=[vmem] * 13, out_spec...  45.2 us
    pallas_call x1, Pallas kernels, reduce_all(): pl.pallas_call(body, out_shape=[jax.ShapeDtypeStruct((width, width), F32)...  39.3 us
    unnamed x30, local copies, waits for them, and re-layouts  13.8 us
    pallas_call x1, Pallas kernels, gather(): pl.pallas_call(gather_kernel, out_shape=[jax.ShapeDtypeStruct((count,) +...  10.2 us

profile of v3, /device:TPU:25, one launch (start us, length us, event | category | flops | bytes accessed | tf_op | source)
XLA Modules:
  0.0 109.8 jit_solution(9324377583355528721)
XLA Ops:
  0.6 0.7 broadcast_in_dim.20.b_in_ref
  1.3 0.0 copy-start
  1.3 0.9 copy-done
  2.2 0.0 copy-start.1
  2.2 0.9 copy-done.1
  3.1 10.2 %gather_weights.1 = (bf16[4,256,256]{2,1,0:T(8,128)(2,1)S(1)}, bf16[4,256,256]{2,1,0:T(8,128)(2,1)S(1)}, f32[4,8,256]{2,1,0:T(8,128)S(1)}) custom-call(bf16[256,256]{1,0:T(8,128)(2,1)S(1)} %copy-done, bf16[256,256]{1,0:T(8,128)(2,1)S(1)} %copy-done.1, bf16[1,256]{1,0:T(2,128)(2,1)S(1)} %broadcast_in_dim.20.b_in_ref), custom_call_target="tpu_custom_call" | custom-call | bytes 33554432 | tf_op jit(solution)/shard_map/gather_weights/pallas_call | solution.py:302
  13.4 0.0 copy-start.2
  13.4 1.6 %copy-done.2 = bf16[32,128,256]{2,1,0:T(8,128)(2,1)S(1)} copy-done((bf16[32,128,256]{2,1,0:T(8,128)(2,1)S(1)}, bf16[32,128,256]{2,1,0:T(8,128)(2,1)}, u32[]{:S(2)}) %copy-start.2) | copy-done | bytes 2097176
  14.9 0.0 copy-start.3
  14.9 0.9 copy-done.3
  15.9 0.0 copy-start.4
  15.9 0.9 copy-done.4
  16.8 0.0 copy-start.5
  16.8 0.8 copy-done.5
  17.6 0.0 copy-start.6
  17.6 0.7 copy-done.6
  18.3 0.0 copy-start.7
  18.3 0.7 copy-done.7
  19.0 0.0 copy-start.8
  19.0 0.7 copy-done.8
  19.7 0.0 copy-start.9
  19.7 0.7 copy-done.9
  20.4 0.0 copy-start.10
  20.4 0.7 copy-done.10
  21.0 0.0 copy-start.11
  21.0 0.7 copy-done.11
  21.7 45.2 %sde.1 = (f32[1,128]{1,0:T(1,128)}, f32[4,576,256]{2,1,0:T(8,128)S(1)}, f32[128,256]{1,0:T(8,128)}) custom-call(f32[128,256]{1,0:T(8,128)S(1)} %copy-done.4, bf16[32,128,256]{2,1,0:T(8,128)(2,1)S(1)} %copy-done.2, f32[1,128]{1,0:T(1,128)S(1)} %bitcast.16, s32[1,128]{1,0:T(1,128)S(1)} %bitcast.17, s32[8,128]{1,0:T(8,128)S(1)} %bitcast.12, ...), custom_call_target="tpu_custom_call" | custom-call | flops 12884901888 | bytes 8388608 | tf_op jit(solution)/shard_map/sde/pallas_call | solution.py:225
  66.9 39.3 %reduce_grads.1 = (f32[256,256]{1,0:T(8,128)S(1)}, f32[256,256]{1,0:T(8,128)S(1)}, f32[1,256]{1,0:T(1,128)S(1)}, f32[1,256]{1,0:T(1,128)S(1)}, f32[256,128]{1,0:T(8,128)S(1)}, /*index=5*/f32[1,2]{1,0:T(1,128)S(1)}) custom-call(f32[4,576,256]{2,1,0:T(8,128)S(1)} %get-tuple-element.24.refs_0_), custom_call_target="tpu_custom_call" | custom-call | tf_op jit(solution)/shard_map/reduce_grads/pallas_call | solution.py:485
  106.1 0.5 copy.27
  106.6 0.7 copy.28
  107.3 0.6 copy.29
  107.9 0.7 copy.30
  108.6 0.6 copy.31
  109.2 0.7 copy.32
Async XLA Ops:
  1.3 0.9 copy-start
  2.2 0.9 copy-start.1
  13.4 1.6 %copy-start.2 = (bf16[32,128,256]{2,1,0:T(8,128)(2,1)S(1)}, bf16[32,128,256]{2,1,0:T(8,128)(2,1)}, u32[]{:S(2)}) copy-start(bf16[32,128,256]{2,1,0:T(8,128)(2,1)} %noise_ref.1) | copy-start | bytes 6291460
  14.9 0.9 copy-start.3
  15.9 0.9 copy-start.4
  16.8 0.8 copy-start.5
  17.6 0.7 copy-start.6
  18.3 0.7 copy-start.7
  19.0 0.7 copy-start.8
  19.7 0.7 copy-start.9
  20.4 0.7 copy-start.10
  21.0 0.7 copy-start.11

commit v4 on v3

--- a/solution.py
+++ b/solution.py
@@ -203,6 +203,28 @@
         jax.ShapeDtypeStruct((chunks, grad_rows, width), F32),
         jax.ShapeDtypeStruct((rows, width), F32),
     ]
+    resident = (6, 7, 8)
+    operands = (init, noise, step, length, obs, seen, w_in, b_in, w_out, b_out, dec, rate, diff)
+    loaded = [i for i in range(len(operands)) if i not in resident]
+    specs = [
+        vmem if i in resident else pl.BlockSpec(memory_space=pltpu.HBM)
+        for i in range(len(operands))
+    ]
+
+    def body(*refs):
+        refs = list(refs)
+        sems = refs.pop()
+        spaces = [refs.pop() for _ in loaded][::-1]
+        copies = []
+        for at, (i, space) in enumerate(zip(loaded, spaces)):
+            copy = pltpu.make_async_copy(refs[i], space, sems.at[at])
+            copy.start()
+            copies.append(copy)
+            refs[i] = space
+        for copy in copies:
+            copy.wait()
+        core_kernel(*refs)
+
     scratch = [
         pltpu.VMEM((steps + 1, rows, width), BF16),
         pltpu.VMEM((width, steps * rows), BF16),
@@ -222,20 +244,22 @@
         pltpu.VMEM((steps * rows, 2 * seen_width), BF16),
         pltpu.VMEM((rows * seen_count, seen_width), F32),
     ]
+    scratch += [pltpu.VMEM(operands[i].shape, operands[i].dtype) for i in loaded]
+    scratch += [pltpu.SemaphoreType.DMA((len(loaded),))]
     return pl.pallas_call(
-        core_kernel,
+        body,
         out_shape=out,
-        in_specs=[vmem] * 13,
+        in_specs=specs,
         out_specs=[vmem] * 3,
         scratch_shapes=scratch,
-        compiler_params=pltpu.CompilerParams(vmem_limit_bytes=44 * 1024 * 1024),
+        compiler_params=pltpu.CompilerParams(vmem_limit_bytes=60 * 1024 * 1024),
         cost_estimate=pl.CostEstimate(
             flops=12 * steps * rows * width * width * chunks,
             bytes_accessed=8 << 20,
             transcendentals=steps * rows * width * chunks,
         ),
         name="sde",
-    )(init, noise, step, length, obs, seen, w_in, b_in, w_out, b_out, dec, rate, diff)
+    )(*operands)
 
 
 def send(source, target, send_sem, recv_sem, peer):
@@ -324,14 +348,9 @@
 def reduce_kernel(
     members,
     total,
-    share,
     grads_ref,
-    w_in_ref,
-    w_out_ref,
-    b_in_ref,
-    b_out_ref,
-    dec_ref,
-    scores_ref,
+    done_ref,
+    decs_ref,
     near_ref,
     far_w_ref,
     far_t_ref,
@@ -340,8 +359,6 @@
     full_ref,
     round_ref,
     parts_ref,
-    done_ref,
-    decs_ref,
     near_send,
     near_recv,
     far_send,
@@ -350,6 +367,8 @@
     rs_recv,
     ag_send,
     ag_recv,
+    pair_send,
+    pair_recv,
     dec_send,
     dec_recv,
 ):
@@ -405,31 +424,44 @@
         scatter[d - 1].wait_recv()
         value = value + parts_ref[d - 1].astype(F32)
     done_ref[here, :] = value / total
+    pair = batch + 1 - 2 * (batch % 2)
+    partner = (pair, mine)
+
+    def rows_of(owner):
+        return done_ref.at[pl.ds(pl.multiple_of(owner * piece, 8), piece), :]
+
+    def relay(i, owner):
+        return send(rows_of(owner), rows_of(owner), pair_send.at[i], pair_recv.at[i], partner)
+
+    hops = members // 2
     spread = []
-    for d in range(1, members):
+    for d in range(1, hops):
+        target = lax.rem(batch + 2 * d, members)
         copy = send(
-            done_ref.at[here, :],
-            done_ref.at[here, :],
+            rows_of(batch), rows_of(batch), ag_send.at[d - 1], ag_recv.at[d - 1], (target, mine)
+        )
+        copy.start()
+        spread.append(copy)
+    passed = [relay(0, batch)]
+    passed[0].start()
+    for copy in near + far + scatter:
+        copy.wait_send()
+    for d in range(1, hops):
+        origin = lax.rem(batch + members - 2 * d, members)
+        send(
+            rows_of(origin),
+            rows_of(origin),
             ag_send.at[d - 1],
             ag_recv.at[d - 1],
-            others[d - 1],
-        )
-        copy.start()
-        spread.append(copy)
-    for copy in near + far + scatter:
-        copy.wait_send()
-    for d in range(1, members):
-        origin = lax.rem(batch + members - d, members)
-        there = pl.ds(pl.multiple_of(origin * piece, 8), piece)
-        send(
-            done_ref.at[there, :],
-            done_ref.at[there, :],
-            ag_send.at[d - 1],
-            ag_recv.at[d - 1],
-            others[d - 1],
+            (origin, mine),
         ).wait_recv()
+        copy = relay(d, origin)
+        copy.start()
+        passed.append(copy)
+    for d in range(hops):
+        relay(d, lax.rem(pair + members - 2 * d, members)).wait_recv()
+    spread += passed
     dec_rows = decs_ref.shape[1]
-    line = weight_rows + dec_rows
     exchange = []
     for i in range(3):
         copy = send(
@@ -441,16 +473,7 @@
         )
         copy.start()
         exchange.append(copy)
-    w_in_ref[...] = done_ref[:width, :]
-    w_out_ref[...] = done_ref[width:weight_rows, :]
-    decs_ref[mine] = done_ref[weight_rows:line, :]
-    b_in_ref[...] = done_ref[line : line + 1, :]
-    b_out_ref[...] = done_ref[line + 1 : line + 2, :]
-    half = share
-    scores_ref[:, 0:1] = jnp.sum(done_ref[line + 2 : line + 3, :half], axis=1, keepdims=True)
-    scores_ref[:, 1:2] = jnp.sum(
-        done_ref[line + 2 : line + 3, half : 2 * half], axis=1, keepdims=True
-    )
+    decs_ref[mine] = done_ref[weight_rows : weight_rows + dec_rows, :]
     for copy in spread:
         copy.wait_send()
     for i, origin in enumerate((sibling, across, diagonal)):
@@ -458,6 +481,23 @@
         send(
             decs_ref.at[origin], decs_ref.at[origin], dec_send.at[i], dec_recv.at[i], group[i]
         ).wait_recv()
+
+
+def finish_kernel(
+    half, done_ref, decs_ref, w_in_ref, w_out_ref, b_in_ref, b_out_ref, dec_ref, scores_ref
+):
+    width = done_ref.shape[1]
+    weight_rows = 2 * width
+    dec_rows = decs_ref.shape[1]
+    line = weight_rows + dec_rows
+    w_in_ref[...] = done_ref[:width, :]
+    w_out_ref[...] = done_ref[width:weight_rows, :]
+    b_in_ref[...] = done_ref[line : line + 1, :]
+    b_out_ref[...] = done_ref[line + 1 : line + 2, :]
+    scores_ref[:, 0:1] = jnp.sum(done_ref[line + 2 : line + 3, :half], axis=1, keepdims=True)
+    scores_ref[:, 1:2] = jnp.sum(
+        done_ref[line + 2 : line + 3, half : 2 * half], axis=1, keepdims=True
+    )
     seen_width = dec_ref.shape[1]
     for n in range(decs_ref.shape[0]):
         for m in range(width // seen_width):
@@ -476,24 +516,20 @@
     piece = grad_rows // members
     vmem = pl.BlockSpec(memory_space=pltpu.VMEM)
     sems = []
-    for count in (2, 2, members - 1, members - 1, 3):
+    for count in (2, 2, members - 1, members // 2, members // 2, 3):
         sems += [pltpu.SemaphoreType.DMA((count,))] * 2
 
     def body(*refs):
-        reduce_kernel(members, total, rows, *refs)
-
-    return pl.pallas_call(
+        reduce_kernel(members, total, *refs)
+
+    done, decs = pl.pallas_call(
         body,
         out_shape=[
-            jax.ShapeDtypeStruct((width, width), F32),
-            jax.ShapeDtypeStruct((width, width), F32),
-            jax.ShapeDtypeStruct((1, width), F32),
-            jax.ShapeDtypeStruct((1, width), F32),
-            jax.ShapeDtypeStruct((width, seen_width), F32),
-            jax.ShapeDtypeStruct((1, 2), F32),
+            jax.ShapeDtypeStruct((grad_rows, width), F32),
+            jax.ShapeDtypeStruct((quarters, dec_rows, width), F32),
         ],
         in_specs=[vmem],
-        out_specs=[vmem] * 6,
+        out_specs=[vmem] * 2,
         scratch_shapes=[
             pltpu.VMEM((2, grad_rows, width), F32),
             pltpu.VMEM((2 * width, width), BF16),
@@ -503,8 +539,6 @@
             pltpu.VMEM((grad_rows, width), F32),
             pltpu.VMEM((members, piece, width), BF16),
             pltpu.VMEM((members - 1, piece, width), BF16),
-            pltpu.VMEM((grad_rows, width), F32),
-            pltpu.VMEM((quarters, dec_rows, width), F32),
         ]
         + sems,
         compiler_params=pltpu.CompilerParams(
@@ -512,6 +546,25 @@
         ),
         name="reduce_grads",
     )(grads)
+
+    def finish(*refs):
+        finish_kernel(rows, *refs)
+
+    return pl.pallas_call(
+        finish,
+        out_shape=[
+            jax.ShapeDtypeStruct((width, width), F32),
+            jax.ShapeDtypeStruct((width, width), F32),
+            jax.ShapeDtypeStruct((1, width), F32),
+            jax.ShapeDtypeStruct((1, width), F32),
+            jax.ShapeDtypeStruct((width, seen_width), F32),
+            jax.ShapeDtypeStruct((1, 2), F32),
+        ],
+        in_specs=[vmem] * 2,
+        out_specs=[vmem] * 6,
+        compiler_params=pltpu.CompilerParams(vmem_limit_bytes=8 * 1024 * 1024),
+        name="finish",
+    )(done, decs)
 
 
 def on_device(

time: 110 us -> 106 us (0.964)
  local copies, waits for them, and re-layouts: 14.5 us -> 6.32 us
  Pallas kernels: 94.7 us -> 98.6 us
    unnamed x30 -> x12, local copies, waits for them, and re-layouts: 13.8 us -> 5.66 us
    pallas_call x2 -> x3, Pallas kernels: 84.4 us -> 88.4 us  [the longest x1 49.6 us: core(): pl.pallas_call(body, out_shape=out, in_specs=specs, out_specs=[vmem] * 3,...]
where the time goes in v4:
time: 106 us
  Pallas kernels  98.6 us (93%)
  local copies, waits for them, and re-layouts  6.32 us (6%)
    pallas_call x1, Pallas kernels, core(): pl.pallas_call(body, out_shape=out, in_specs=specs, out_specs=[vmem] * 3,...  49.6 us
    pallas_call x1, Pallas kernels, reduce_all(): pl.pallas_call(body, out_shape=[jax.ShapeDtypeStruct((grad_rows, width),...  37.9 us
    pallas_call x1, Pallas kernels, gather(): pl.pallas_call(gather_kernel, out_shape=[jax.ShapeDtypeStruct((count,) +...  10.2 us
    unnamed x12, local copies, waits for them, and re-layouts  5.66 us

profile of v4, /device:TPU:25, one launch (start us, length us, event | category | flops | bytes accessed | tf_op | source)
XLA Modules:
  0.0 105.6 jit_solution(6791156246216542246)
XLA Ops:
  0.6 0.7 broadcast_in_dim.20.b_in_ref
  1.3 0.0 copy-start.1
  1.3 0.9 copy-done.1
  2.2 0.0 copy-start.2
  2.2 0.9 copy-done.2
  3.1 10.2 %gather_weights.1 = (bf16[4,256,256]{2,1,0:T(8,128)(2,1)S(1)}, bf16[4,256,256]{2,1,0:T(8,128)(2,1)S(1)}, f32[4,8,256]{2,1,0:T(8,128)S(1)}) custom-call(bf16[256,256]{1,0:T(8,128)(2,1)S(1)} %copy-done.1, bf16[256,256]{1,0:T(8,128)(2,1)S(1)} %copy-done.2, bf16[1,256]{1,0:T(2,128)(2,1)S(1)} %broadcast_in_dim.20.b_in_ref), custom_call_target="tpu_custom_call" | custom-call | bytes 33554432 | tf_op jit(solution)/shard_map/gather_weights/pallas_call | solution.py:326
  13.4 0.0 copy-start.3
  13.4 0.8 copy-done.3
  14.1 0.0 copy-start.4
  14.1 0.8 copy-done.4
  14.9 0.0 copy-start.5
  14.9 0.6 copy-done.5
  15.6 49.6 %sde.1 = (f32[1,128]{1,0:T(1,128)}, f32[4,576,256]{2,1,0:T(8,128)}, f32[128,256]{1,0:T(8,128)}) custom-call(f32[128,256]{1,0:T(8,128)} %refs_0_.1, bf16[32,128,256]{2,1,0:T(8,128)(2,1)} %refs_1_.1, f32[1,128]{1,0:T(1,128)} %bitcast.16, s32[1,128]{1,0:T(1,128)} %bitcast.17, s32[8,128]{1,0:T(8,128)} %bitcast.10, bf16[128,8,128]{2,1,0:T(8,128)(2,1)} %refs_5_.1, ...), custom_call_target="tpu_custom_call" | custom-call | flops 12884901888 | bytes 8388608 | tf_op jit(solution)/shard_map/sde/pallas_call | solution.py:249
  65.2 0.0 copy-start
  65.2 1.7 %copy-done = f32[4,576,256]{2,1,0:T(8,128)S(1)} copy-done((f32[4,576,256]{2,1,0:T(8,128)S(1)}, f32[4,576,256]{2,1,0:T(8,128)}, u32[]{:S(2)}) %copy-start) | copy-done | bytes 2359320
  66.9 37.9 %reduce_grads.1 = (f32[576,256]{1,0:T(8,128)S(1)}, f32[4,32,256]{2,1,0:T(8,128)S(1)}) custom-call(f32[4,576,256]{2,1,0:T(8,128)S(1)} %copy-done), custom_call_target="tpu_custom_call" | custom-call | tf_op jit(solution)/shard_map/reduce_grads/pallas_call | solution.py:525
  104.8 0.9 finish.1
Async XLA Ops:
  1.3 0.9 copy-start.1
  2.2 0.9 copy-start.2
  13.4 0.8 copy-start.3
  14.1 0.8 copy-start.4
  14.9 0.6 copy-start.5
  65.2 1.7 %copy-start = (f32[4,576,256]{2,1,0:T(8,128)S(1)}, f32[4,576,256]{2,1,0:T(8,128)}, u32[]{:S(2)}) copy-start(f32[4,576,256]{2,1,0:T(8,128)} %get-tuple-element.26.refs_0_) | copy-start | bytes 7077892

commit v5 on v4

--- a/solution.py
+++ b/solution.py
@@ -135,7 +135,10 @@
         low = (total - high.astype(F32)).astype(BF16)
         miss_ref[pl.ds(k * rows, rows), :seen_width] = high
         miss_ref[pl.ds(k * rows, rows), seen_width:] = low
-        obs_back = dot_nt(high, dec_ref[...]) + dot_nt(low, dec_ref[...])
+        obs_back = dot_nt(
+            jnp.concatenate([high, low], axis=1),
+            jnp.concatenate([dec_ref[...], dec_ref[...]], axis=1),
+        )
         cot = cot_ref[...] + obs_back
         scaled = scaled_ref[k]
         factor = both(jnp.where(k < len_ref[...], dt_ref[...], 0.0))
@@ -338,7 +341,7 @@
             pltpu.SemaphoreType.DMA((3, 3)),
         ],
         compiler_params=pltpu.CompilerParams(
-            collective_id=0, has_side_effects=True, vmem_limit_bytes=8 * 1024 * 1024
+            collective_id=0, has_side_effects=True, vmem_limit_bytes=60 * 1024 * 1024
         ),
         cost_estimate=pl.CostEstimate(flops=0, bytes_accessed=32 << 20, transcendentals=0),
         name="gather_weights",
@@ -542,7 +545,7 @@
         ]
         + sems,
         compiler_params=pltpu.CompilerParams(
-            collective_id=1, has_side_effects=True, vmem_limit_bytes=16 * 1024 * 1024
+            collective_id=1, has_side_effects=True, vmem_limit_bytes=60 * 1024 * 1024
         ),
         name="reduce_grads",
     )(grads)

time: 106 us -> 108 us (1.019)
  Pallas kernels: 98.6 us -> 104 us
  local copies, waits for them, and re-layouts: 6.32 us -> 3.18 us
    unnamed x12 -> x4, local copies, waits for them, and re-layouts: 5.66 us -> 1.96 us
    pallas_call x1, Pallas kernels: 37.9 us -> 40.5 us  [reduce_all(): pl.pallas_call(body, out_shape=[jax.ShapeDtypeStruct((grad_rows, width),...]
    pallas_call x1, Pallas kernels: 10.2 us -> 12.2 us  [gather(): pl.pallas_call(gather_kernel, out_shape=[jax.ShapeDtypeStruct((count,) +...]
where the time goes in v5:
time: 108 us
  Pallas kernels  104 us (96%)
  local copies, waits for them, and re-layouts  3.18 us (3%)
    pallas_call x1, Pallas kernels, core(): pl.pallas_call(body, out_shape=out, in_specs=specs, out_specs=[vmem] * 3,...  50.4 us
    pallas_call x1, Pallas kernels, reduce_all(): pl.pallas_call(body, out_shape=[jax.ShapeDtypeStruct((grad_rows, width),...  40.5 us
    pallas_call x1, Pallas kernels, gather(): pl.pallas_call(gather_kernel, out_shape=[jax.ShapeDtypeStruct((count,) +...  12.2 us

profile of v5, /device:TPU:25, one launch (start us, length us, event | category | flops | bytes accessed | tf_op | source)
XLA Modules:
  0.0 107.8 jit_solution(521854636245623284)
XLA Ops:
  0.6 1.2 %broadcast_in_dim.20.b_in_ref = bf16[1,256]{1,0:T(2,128)(2,1)} reshape(bf16[256]{0:T(256)(128)(2,1)} %param.20) | data formatting | bytes 1024 | tf_op jit(solution)/shard_map/broadcast_in_dim | solution.py:590
  1.9 12.2 %gather_weights.1 = (bf16[4,256,256]{2,1,0:T(8,128)(2,1)}, bf16[4,256,256]{2,1,0:T(8,128)(2,1)}, f32[4,8,256]{2,1,0:T(8,128)}) custom-call(bf16[256,256]{1,0:T(8,128)(2,1)} %w_in_ref.1, bf16[256,256]{1,0:T(8,128)(2,1)} %w_out_ref.1, bf16[1,256]{1,0:T(2,128)(2,1)} %broadcast_in_dim.20.b_in_ref), custom_call_target="tpu_custom_call" | custom-call | bytes 33554432 | tf_op jit(solution)/shard_map/gather_weights/pallas_call | solution.py:329
  14.0 50.4 %sde.1 = (f32[1,128]{1,0:T(1,128)}, f32[4,576,256]{2,1,0:T(8,128)}, f32[128,256]{1,0:T(8,128)}) custom-call(f32[128,256]{1,0:T(8,128)} %refs_0_.1, bf16[32,128,256]{2,1,0:T(8,128)(2,1)} %refs_1_.1, f32[1,128]{1,0:T(1,128)} %bitcast.16, s32[1,128]{1,0:T(1,128)} %bitcast.17, s32[8,128]{1,0:T(8,128)} %bitcast.10, bf16[128,8,128]{2,1,0:T(8,128)(2,1)} %refs_5_.1, ...), custom_call_target="tpu_custom_call" | custom-call | flops 12884901888 | bytes 8388608 | tf_op jit(solution)/shard_map/sde/pallas_call | solution.py:252
  64.5 40.5 %reduce_grads.1 = (f32[576,256]{1,0:T(8,128)}, f32[4,32,256]{2,1,0:T(8,128)}) custom-call(f32[4,576,256]{2,1,0:T(8,128)} %get-tuple-element.26.refs_0_), custom_call_target="tpu_custom_call" | custom-call | tf_op jit(solution)/shard_map/reduce_grads/pallas_call | solution.py:528
  104.9 0.0 copy-start
  104.9 1.1 copy-done
  106.0 0.0 copy-start.1
  106.0 0.9 copy-done.1
  106.9 0.9 finish.1
Async XLA Ops:
  104.9 1.1 copy-start
  106.0 0.9 copy-start.1
